TPU v7x, 128 devices: a whole 4x4x4 slice. The times are simulated.
128 devices in a mesh: grp: 4 (over x), tile: 32 (over y, z, core).
Axes of the slice: x: 4, y: 4, z: 4, core: 2. Of those that a mesh axis runs over, the one named last changes fastest.
Arguments:
- descriptors: bfloat16 [64, 4096, 256], P('grp', 'tile'), may hold values from -8 to 8
- pairs: int32 [32, 2], P('grp'), may hold values from 0 to 63, as said below
- counts: int32 [64], replicated, may hold values from 1024 to 4096
Outputs:
- row_lse: float32 [32, 4096], P('grp', 'tile')
- col_lse: float32 [32, 4096], P('grp', 'tile')
- best_log: float32 [32, 4096], P('grp', 'tile')
Inputs may be any that keep to these rules, and one draw needn't show every extreme that they name: `pairs`: the two images of a pair differ.
All inputs are finite; a program needn't handle non-finite values.
Results may differ from a plain program's by a relative error of at most 0.0003.
Values may be sent and summed in bfloat16 or wider, within the bound.
A program may use at most 64 MiB of HBM per device.

v0:
```python
import math
import jax
import jax.numpy as jnp
from jax import lax
from jax.sharding import Mesh
from jax.sharding import PartitionSpec as P

QBLK = 4
TILE = ("tile_0", "tile_1", "tile_2")
NEGATIVE = -1e30


def in_one_piece(arrays, axis, split_dim, concat_dim, along):
    both = jnp.concatenate(arrays, axis=along)
    out, at, outs = (
        lax.all_to_all(both, axis, split_axis=split_dim, concat_axis=concat_dim, tiled=True),
        0,
        [],
    )
    for a in arrays:
        outs.append(lax.slice_in_dim(out, at, at + a.shape[along], axis=along))
        at += a.shape[along]
    return tuple(outs)


def in_blocks(value, dim, count):
    lengths = value.shape
    tiles = value.reshape(*lengths[:dim], count, lengths[dim] // count, *lengths[dim + 1 :])
    return jnp.moveaxis(tiles, dim, 0)


def joined_along(tiles, dim):
    lengths = list(tiles.shape[1:])
    lengths[dim] *= tiles.shape[0]
    return jnp.moveaxis(tiles, 0, dim).reshape(lengths)


def exchange_in_order(tiles, axes, turns):
    inside = tiles.shape[1:]
    out = tiles.reshape(*(lax.axis_size(a) for a in axes), *inside)
    for k in turns:
        out = lax.all_to_all(out, axes[k], k, k, tiled=True)
    return out.reshape(-1, *inside)


def core_and_chips(value, groups, turns, split_dim, concat_dim):
    count = lax.axis_size(groups[0]) * lax.axis_size(groups[1])
    tiles = in_blocks(value, split_dim, count)
    return joined_along(exchange_in_order(tiles, groups, turns), concat_dim)


def join_stats(earlier, later):
    highest = jnp.maximum(earlier[0], later[0])
    summed = earlier[1] * jnp.exp(earlier[0] - highest) + later[1] * jnp.exp(later[0] - highest)
    return (highest, summed)


def slot_first(item, query_index, score_scale):
    query_rows, key_image, query_count, key_count = item
    height = query_rows.shape[0]
    width = query_rows.shape[1]
    total_keys = key_image.shape[0]
    block = min(512, height)
    number = height // block
    key_mask = (lax.iota(jnp.int32, total_keys) < key_count)[None, :]
    grouped = query_rows.reshape(number, block, width)
    index_groups = query_index.reshape(number, block)

    def first_pass(carried, inputs):
        block_rows, block_index = inputs
        scores = (
            jnp.einsum("qd,kd->qk", block_rows, key_image, preferred_element_type=jnp.float32)
            * score_scale
        )
        query_mask = (block_index < query_count)[:, None]
        row_top = jnp.max(jnp.where(key_mask, scores, NEGATIVE), axis=1)
        row_total = jnp.sum(jnp.where(key_mask, jnp.exp(scores - row_top[:, None]), 0.0), axis=1)
        col_top = jnp.max(jnp.where(query_mask, scores, NEGATIVE), axis=0)
        col_total = jnp.sum(jnp.where(query_mask, jnp.exp(scores - col_top[None, :]), 0.0), axis=0)
        return (join_stats(carried, (col_top, col_total)), row_top + jnp.log(row_total))

    start_stats = (
        jnp.full((total_keys,), NEGATIVE, jnp.float32),
        jnp.zeros((total_keys,), jnp.float32),
    )
    col_stats, row_values = lax.scan(first_pass, start_stats, (grouped, index_groups))
    return (col_stats[0], col_stats[1], row_values.reshape(height))


def slot_second(item, query_index, score_scale):
    query_rows, key_image, row_values, col_values, query_count, key_count = item
    height = query_rows.shape[0]
    width = query_rows.shape[1]
    total_keys = key_image.shape[0]
    block = min(512, height)
    number = height // block
    key_mask = (lax.iota(jnp.int32, total_keys) < key_count)[None, :]
    grouped = query_rows.reshape(number, block, width)
    lse_groups = row_values.reshape(number, block)

    def second_pass(carried, inputs):
        block_rows, block_lse = inputs
        scores = (
            jnp.einsum("qd,kd->qk", block_rows, key_image, preferred_element_type=jnp.float32)
            * score_scale
        )
        best = (
            jnp.max(jnp.where(key_mask, 2.0 * scores - col_values[None, :], NEGATIVE), axis=1)
            - block_lse
        )
        return (carried, best)

    unused, best_values = lax.scan(second_pass, jnp.int32(0), (grouped, lse_groups))
    query_valid = query_index < query_count
    return (
        jnp.where(query_valid, row_values, 0.0),
        jnp.where(query_valid, best_values.reshape(height), 0.0),
    )


def paired_blocks(queries, keys_local, query_counts, key_counts, score_scale):
    devices_here = lax.axis_size(TILE)
    rows = queries.shape[1]
    width = queries.shape[2]
    slots = devices_here // QBLK
    sub = rows // QBLK
    pair_count = queries.shape[0]
    per_slot = -(-pair_count // slots)
    padded = per_slot * slots
    query_send = (
        queries.reshape(slots, per_slot, QBLK, sub, width)
        .transpose(0, 2, 1, 3, 4)
        .reshape(devices_here, per_slot, sub, width)
    )
    key_send = jnp.broadcast_to(
        keys_local.reshape(slots, 1, per_slot, rows, width), (slots, QBLK, per_slot, rows, width)
    ).reshape(devices_here, per_slot, rows, width)
    query_got, key_got = in_one_piece((query_send, key_send), TILE, 0, 0, 2)
    query_here = query_got.transpose(1, 0, 2, 3).reshape(per_slot, devices_here * sub, width)
    key_here = key_got.transpose(1, 0, 2, 3).reshape(per_slot, devices_here * rows, width)
    place = lax.axis_index(TILE)
    slot = place // QBLK
    quarter = place % QBLK
    query_index = (
        lax.iota(jnp.int32, devices_here)[:, None] * rows
        + quarter * sub
        + lax.iota(jnp.int32, sub)[None, :]
    ).reshape(devices_here * sub)
    query_own = lax.dynamic_slice_in_dim(query_counts, slot * per_slot, per_slot, 0)
    key_own = lax.dynamic_slice_in_dim(key_counts, slot * per_slot, per_slot, 0)
    col_top, col_total, row_values = lax.map(
        lambda item: slot_first(item, query_index, score_scale),
        (query_here, key_here, query_own, key_own),
    )

    def by_block(values):
        return values.reshape(per_slot, devices_here, rows).transpose(1, 0, 2)

    top_got, total_got = in_one_piece((by_block(col_top), by_block(col_total)), TILE, 0, 0, 1)
    top_got = top_got.reshape(slots, QBLK, per_slot, rows)
    total_got = total_got.reshape(slots, QBLK, per_slot, rows)
    stats = (top_got[:, 0], total_got[:, 0])
    for member in range(1, QBLK):
        stats = join_stats(stats, (top_got[:, member], total_got[:, member]))
    col_block = stats[0] + jnp.log(stats[1])
    col_send = jnp.broadcast_to(col_block[:, None], (slots, QBLK, per_slot, rows)).reshape(
        devices_here, per_slot, rows
    )
    col_got = core_and_chips(col_send, (("tile_0", "tile_1"), "tile_2"), (1, 0), 0, 0)
    col_values = col_got.transpose(1, 0, 2).reshape(per_slot, devices_here * rows)
    row_out, best_out = lax.map(
        lambda item: slot_second(item, query_index, score_scale),
        (query_here, key_here, row_values, col_values, query_own, key_own),
    )

    def to_owner(values):
        return values.reshape(per_slot, devices_here, sub).transpose(1, 0, 2)

    row_got, best_got = (
        lax.all_to_all(to_owner(row_out), TILE, split_axis=0, concat_axis=0, tiled=True),
        lax.all_to_all(to_owner(best_out), TILE, split_axis=0, concat_axis=0, tiled=True),
    )

    def from_slots(values):
        return (
            values.reshape(slots, QBLK, per_slot, sub).transpose(0, 2, 1, 3).reshape(padded, rows)
        )

    key_place = place * rows + lax.iota(jnp.int32, rows)
    key_valid_own = key_place[None, :] < key_counts[:, None]
    col_out = jnp.where(key_valid_own, col_block.reshape(padded, rows), 0.0)
    return (from_slots(row_got), col_out, from_slots(best_got))


def local(descriptors, pairs, counts):
    score_scale = 2.0 / math.sqrt(descriptors.shape[2])
    image_rows = lax.all_gather(descriptors, "grp", axis=0, tiled=True)
    image_ids = lax.iota(jnp.int32, counts.shape[0])
    first_image = pairs[:, 0]
    second = pairs[:, 1]
    query_counts = jnp.sum(
        jnp.where(first_image[:, None] == image_ids[None, :], counts[None, :], 0), axis=1
    )
    key_counts = jnp.sum(
        jnp.where(second[:, None] == image_ids[None, :], counts[None, :], 0), axis=1
    )
    queries = jnp.take(image_rows, first_image, axis=0)
    keys_local = jnp.take(image_rows, second, axis=0)
    return paired_blocks(queries, keys_local, query_counts, key_counts, score_scale)


def solution(mesh):
    torus = Mesh(
        mesh.devices.reshape(mesh.shape["grp"], 4, 4, 2), ("grp", "tile_0", "tile_1", "tile_2")
    )
    return jax.shard_map(
        local,
        mesh=torus,
        in_specs=(P("grp", TILE, None), P("grp", None), P()),
        out_specs=(P("grp", TILE), P("grp", TILE), P("grp", TILE)),
        check_vma=False,
    )
```

profile of v0, /device:TPU:1, one launch (start us, length us, event | category | flops | bytes accessed | tf_op | source)
XLA Modules:
  0.0 198.5 jit_solution(10425971025592148428)
XLA Ops:
  7.2 0.7 all-gather.2.cloned.1.call-update
  7.9 0.8 compare_and_fusion.1
  8.7 52.2 %all-gather.2.cloned.1.call-done = bf16[64,128,256]{2,1,0:T(8,128)(2,1)} async-done(((bf16[16,128,256]{2,1,0:T(8,128)(2,1)}), bf16[64,128,256]{2,1,0:T(8,128)(2,1)}) %all-gather.2.cloned.1.call-update) | async-done | bytes 4194320 | tf_op jit(solution)/shard_map/all_gather | solution.py:197
  60.9 2.8 %gather_fusion = bf16[8,128,256]{2,1,0:T(8,128)(2,1)S(1)} fusion(bf16[64,128,256]{2,1,0:T(8,128)(2,1)} %all-gather.2.cloned.1.call-done, s32[1024]{0:T(1024)S(1)} %pad_clamp_fusion.1), kind=kCustom, calls=%fused_computation.clone | custom fusion | bytes 1048608 | tf_op jit(solution)/shard_map/jit(_take)/gather | solution.py:207
  63.7 2.8 %gather_fusion.1 = bf16[8,128,256]{2,1,0:T(8,128)(2,1)S(1)} fusion(bf16[64,128,256]{2,1,0:T(8,128)(2,1)} %all-gather.2.cloned.1.call-done, s32[1024]{0:T(1024)S(1)} %pad_clamp_fusion), kind=kCustom, calls=%fused_computation.1.clone | custom fusion | bytes 1048608 | tf_op jit(solution)/shard_map/jit(_take)/gather | solution.py:208
  66.5 0.2 broadcast_select_fusion
  66.6 0.2 broadcast_in_dim.140
  66.9 1.7 pad_maximum_fusion
  68.6 7.9 %all-to-all-start = ((bf16[32,1,160,256]{3,2,1,0:T(8,128)(2,1)}), bf16[32,1,160,256]{3,2,1,0:T(8,128)(2,1)S(1)}, u32[]{:S(2)}, u32[]{:S(2)}) async-start(bf16[32,1,160,256]{3,2,1,0:T(8,128)(2,1)} %pad_maximum_fusion), calls=%async_computation | async-start | bytes 5242880 | tf_op jit(solution)/shard_map/all_to_all | solution.py:16
  76.5 0.2 select_reduce_fusion.5
  76.8 0.6 dynamic_slice.52
  77.4 0.6 dynamic_slice.53
  78.0 0.1 add.160
  78.1 0.1 add.162
  78.2 32.2 %all-to-all-done = bf16[32,1,160,256]{3,2,1,0:T(8,128)(2,1)S(1)} async-done(((bf16[32,1,160,256]{3,2,1,0:T(8,128)(2,1)}), bf16[32,1,160,256]{3,2,1,0:T(8,128)(2,1)S(1)}, u32[]{:S(2)}, u32[]{:S(2)}) %all-to-all-start) | async-done | bytes 2621472 | tf_op jit(solution)/shard_map/all_to_all | solution.py:16
  110.4 1.5 slice.61
  112.0 20.6 %while.48 = (s32[]{:T(128)}, f32[4096]{0:T(1024)S(1)}, f32[4096]{0:T(1024)S(1)}, f32[2,512]{1,0:T(2,128)S(1)}, s32[2,512]{1,0:T(2,128)S(1)}, /*index=5*/s32[]{:T...) while((s32[]{:T(128)}, f32[4096]{0:T(1024)S(1)}, ...), condition=%wide.region_7.9_spmd.clone, body=%wide.region_2.8_spmd.clone.sunk | while | flops 1098936320 | bytes 19316360 | solution.py:86
  112.0 0.7 compare_reduce_fusion.8
  112.6 0.7 compare_reduce_fusion.7
  113.3 4.0 %select_reduce_fusion.11 = (f32[512]{0:T(512)S(1)}, f32[4096]{0:T(1024)S(1)}, f32[512,4096]{1,0:T(8,128)S(1)}) fusion(pred[4096]{0:T(1024)(128)(4,1)S(1)} %compare_reduce_fusion.7, pred[512]{0:T(512)(128)(4,1)S(1)} %compare_reduce_fusion.8, bf16[4096,256]{1,0:T(8,128)(2,1)} %get-tuple-element.457, bf16[2,512,256]{2,1,0:T(8,128)(2,1)S(1)} %get-tuple-element.456, ...), kind=kOutput, calls=%fused_computation.11.clone.1 | convolution fusion | flops 1084222976 | bytes 10770948 | tf_op jit(solution)/shard_map/while/body/eval_jaxpr/while/body/eval_jaxpr/qd,kd->qk/dot_general | solution.py:72
  117.3 4.8 %select_reduce_fusion.12 = (f32[512]{0:T(512)S(1)}, f32[4096]{0:T(1024)S(1)}) fusion(f32[512,4096]{1,0:T(8,128)S(1)} %get-tuple-element.421, f32[512]{0:T(512)S(1)} %get-tuple-element.422, pred[4096]{0:T(1024)(128)(4,1)S(1)} %compare_reduce_fusion.7, f32[4096]{0:T(1024)S(1)} %get-tuple-element.423, pred[512]{0:T(512)(128)(4,1)S(1)} %compare_reduce_fusion.8), kind=kLoop, calls=%fused_computation.10.clone.1 | loop fusion | flops 14675456 | bytes 8430080 | tf_op jit(solution)/shard_map/while/body/eval_jaxpr/while/body/eval_jaxpr/reduce_sum | solution.py:77
  122.3 0.7 compare_reduce_fusion.8
  122.9 0.7 compare_reduce_fusion.7
  123.6 3.9 %select_reduce_fusion.11 = (f32[512]{0:T(512)S(1)}, f32[4096]{0:T(1024)S(1)}, f32[512,4096]{1,0:T(8,128)S(1)}) fusion(pred[4096]{0:T(1024)(128)(4,1)S(1)} %compare_reduce_fusion.7, pred[512]{0:T(512)(128)(4,1)S(1)} %compare_reduce_fusion.8, bf16[4096,256]{1,0:T(8,128)(2,1)} %get-tuple-element.457, bf16[2,512,256]{2,1,0:T(8,128)(2,1)S(1)} %get-tuple-element.456, ...), kind=kOutput, calls=%fused_computation.11.clone.1 | convolution fusion | flops 1084222976 | bytes 10770948 | tf_op jit(solution)/shard_map/while/body/eval_jaxpr/while/body/eval_jaxpr/qd,kd->qk/dot_general | solution.py:72
  127.6 4.8 %select_reduce_fusion.12 = (f32[512]{0:T(512)S(1)}, f32[4096]{0:T(1024)S(1)}) fusion(f32[512,4096]{1,0:T(8,128)S(1)} %get-tuple-element.421, f32[512]{0:T(512)S(1)} %get-tuple-element.422, pred[4096]{0:T(1024)(128)(4,1)S(1)} %compare_reduce_fusion.7, f32[4096]{0:T(1024)S(1)} %get-tuple-element.423, pred[512]{0:T(512)(128)(4,1)S(1)} %compare_reduce_fusion.8), kind=kLoop, calls=%fused_computation.10.clone.1 | loop fusion | flops 14675456 | bytes 8430080 | tf_op jit(solution)/shard_map/while/body/eval_jaxpr/while/body/eval_jaxpr/reduce_sum | solution.py:77
  132.6 11.1 %all_to_all.30 = f32[32,2,128]{2,1,0:T(2,128)S(1)} all-to-all(f32[32,2,128]{2,1,0:T(2,128)S(1)} %pad_maximum_fusion.1), channel_id=1, replica_groups=mesh['grp'=4,'tile_0'=4,'tile_1'=4,'tile_2'=2] {'tile_0','tile_1','tile_2'}, dimensions={0} | all-to-all | bytes 65536 | tf_op jit(solution)/shard_map/all_to_all | solution.py:16
  143.8 3.8 %all_to_all.31 = f32[16,2,1,1,128]{4,3,2,0,1:T(1,128)S(1)} all-to-all(f32[16,2,1,1,128]{4,3,2,0,1:T(1,128)S(1)} %broadcast_in_dim.147), channel_id=1, replica_groups=mesh['grp'=4,'tile_0'=4,'tile_1'=4,'tile_2'=2] {'tile_2'}, dimensions={1} | all-to-all | bytes 32768 | tf_op jit(solution)/shard_map/all_to_all | solution.py:42
  147.5 0.6 copy.107
  148.1 3.5 %all-to-all-start.4 = ((f32[16,2,1,1,128]{4,3,2,1,0:T(1,128)}), f32[16,2,1,1,128]{4,3,2,1,0:T(1,128)S(1)}, u32[]{:S(2)}, u32[]{:S(2)}) async-start(f32[16,2,1,1,128]{4,3,2,1,0:T(1,128)} %copy.107), calls=%async_computation.4 | async-start | bytes 32768 | tf_op jit(solution)/shard_map/all_to_all | solution.py:42
  151.7 0.1 squeeze.81
  151.8 6.3 %all-to-all-done.4 = f32[16,2,1,1,128]{4,3,2,1,0:T(1,128)S(1)} async-done(((f32[16,2,1,1,128]{4,3,2,1,0:T(1,128)}), f32[16,2,1,1,128]{4,3,2,1,0:T(1,128)S(1)}, u32[]{:S(2)}, u32[]{:S(2)}) %all-to-all-start.4) | async-done | bytes 16416 | tf_op jit(solution)/shard_map/all_to_all | solution.py:42
  158.0 7.6 %while.47 = (s32[]{:T(128)}, f32[2,512]{1,0:T(2,128)S(1)}, bf16[2,512,256]{2,1,0:T(8,128)(2,1)S(1)}, bf16[4096,256]{1,0:T(8,128)(2,1)}, f32[4096]{0:T(1024)S(1)}...) while((s32[]{:T(128)}, f32[2,512]{1,0:T(2,128)S(1)}, ...), condition=%wide.region_10.12_spmd.clone, body=%wide.region_8.11_spmd.clone.sunk | while | flops 1082134528 | bytes 2396269 | solution.py:113
  158.0 0.7 compare_reduce_fusion.6
  158.7 3.0 %select_reduce_fusion.10 = f32[512]{0:T(512)S(1)} fusion(bf16[4096,256]{1,0:T(8,128)(2,1)} %get-tuple-element.482, f32[4096]{0:T(1024)S(1)} %get-tuple-element.483, pred[4096]{0:T(1024)(128)(4,1)S(1)} %compare_reduce_fusion.6, bf16[2,512,256]{2,1,0:T(8,128)(2,1)S(1)} %get-tuple-element.481, s32[]{:T(128)} %get-tuple-element.470), kind=kOutput, calls=%fused_computation.4.clone.1 | convolution fusion | flops 1082129920 | bytes 2381828 | tf_op jit(solution)/shard_map/while/body/eval_jaxpr/while/body/eval_jaxpr/qd,kd->qk/dot_general | solution.py:104
  161.8 0.7 compare_reduce_fusion.6
  162.5 3.0 %select_reduce_fusion.10 = f32[512]{0:T(512)S(1)} fusion(bf16[4096,256]{1,0:T(8,128)(2,1)} %get-tuple-element.482, f32[4096]{0:T(1024)S(1)} %get-tuple-element.483, pred[4096]{0:T(1024)(128)(4,1)S(1)} %compare_reduce_fusion.6, bf16[2,512,256]{2,1,0:T(8,128)(2,1)S(1)} %get-tuple-element.481, s32[]{:T(128)} %get-tuple-element.470), kind=kOutput, calls=%fused_computation.4.clone.1 | convolution fusion | flops 1082129920 | bytes 2381828 | tf_op jit(solution)/shard_map/while/body/eval_jaxpr/while/body/eval_jaxpr/qd,kd->qk/dot_general | solution.py:104
  165.6 0.1 reshape.246
  165.7 1.4 compare_select_fusion
  167.1 4.9 %all-to-all-start.1 = ((f32[32,1,32]{2,1,0:T(1,128)}), f32[32,1,32]{2,1,0:T(1,128)S(1)}, u32[]{:S(2)}, u32[]{:S(2)}) async-start(f32[32,1,32]{2,1,0:T(1,128)} %get-tuple-element.313), calls=%async_computation.1 | async-start | bytes 32768 | tf_op jit(solution)/shard_map/all_to_all | solution.py:180
  172.0 7.1 %all-to-all-done.1 = f32[32,1,32]{2,1,0:T(1,128)S(1)} async-done(((f32[32,1,32]{2,1,0:T(1,128)}), f32[32,1,32]{2,1,0:T(1,128)S(1)}, u32[]{:S(2)}, u32[]{:S(2)}) %all-to-all-start.1) | async-done | bytes 4128 | tf_op jit(solution)/shard_map/all_to_all | solution.py:180
  179.1 4.2 %all-to-all-start.5 = ((f32[32,1,32]{2,1,0:T(1,128)}), f32[32,1,32]{2,1,0:T(1,128)S(1)}, u32[]{:S(2)}, u32[]{:S(2)}) async-start(f32[32,1,32]{2,1,0:T(1,128)} %get-tuple-element.312), calls=%async_computation.5 | async-start | bytes 32768 | tf_op jit(solution)/shard_map/all_to_all | solution.py:181
  183.2 0.7 add_select_fusion
  183.9 0.5 broadcast.199
  184.4 0.7 reduce.12
  185.1 0.7 reshape_transpose_reshape.10
  185.8 4.5 %all-to-all-done.5 = f32[32,1,32]{2,1,0:T(1,128)S(1)} async-done(((f32[32,1,32]{2,1,0:T(1,128)}), f32[32,1,32]{2,1,0:T(1,128)S(1)}, u32[]{:S(2)}, u32[]{:S(2)}) %all-to-all-start.5) | async-done | bytes 4128 | tf_op jit(solution)/shard_map/all_to_all | solution.py:181
  190.3 0.7 reduce.13
  191.0 0.7 reshape_transpose_reshape.11
  (36 shorter events, 0.6 us)
Async XLA Ops:
  7.2 53.7 %all-gather.2.cloned.1.call-start = ((), (), s32[]{:S(2)}) async-start(), calls=%async_computation.6 | async-start | bytes 5242880 | tf_op jit(solution)/shard_map/all_gather | solution.py:197
  63.6 12.9 %copy-start = (s32[8,2]{0,1:T(2,128)S(1)}, s32[8,2]{0,1:T(2,128)}, u32[]{:S(2)}) copy-start(s32[8,2]{0,1:T(2,128)} %param.10) | copy-start | bytes 196
  63.7 12.9 %copy-start.1 = (s32[64]{0:T(128)S(1)}, s32[64]{0:T(128)}, u32[]{:S(2)}) copy-start(s32[64]{0:T(128)} %param.11) | copy-start | bytes 772
  68.6 41.8 %all-to-all-start = ((bf16[32,1,160,256]{3,2,1,0:T(8,128)(2,1)}), bf16[32,1,160,256]{3,2,1,0:T(8,128)(2,1)S(1)}, u32[]{:S(2)}, u32[]{:S(2)}) async-start(bf16[32,1,160,256]{3,2,1,0:T(8,128)(2,1)} %pad_maximum_fusion), calls=%async_computation | async-start | bytes 5242880 | tf_op jit(solution)/shard_map/all_to_all | solution.py:16
  148.1 9.9 %all-to-all-start.4 = ((f32[16,2,1,1,128]{4,3,2,1,0:T(1,128)}), f32[16,2,1,1,128]{4,3,2,1,0:T(1,128)S(1)}, u32[]{:S(2)}, u32[]{:S(2)}) async-start(f32[16,2,1,1,128]{4,3,2,1,0:T(1,128)} %copy.107), calls=%async_computation.4 | async-start | bytes 32768 | tf_op jit(solution)/shard_map/all_to_all | solution.py:42
  167.1 12.0 %all-to-all-start.1 = ((f32[32,1,32]{2,1,0:T(1,128)}), f32[32,1,32]{2,1,0:T(1,128)S(1)}, u32[]{:S(2)}, u32[]{:S(2)}) async-start(f32[32,1,32]{2,1,0:T(1,128)} %get-tuple-element.313), calls=%async_computation.1 | async-start | bytes 32768 | tf_op jit(solution)/shard_map/all_to_all | solution.py:180
  179.1 11.2 %all-to-all-start.5 = ((f32[32,1,32]{2,1,0:T(1,128)}), f32[32,1,32]{2,1,0:T(1,128)S(1)}, u32[]{:S(2)}, u32[]{:S(2)}) async-start(f32[32,1,32]{2,1,0:T(1,128)} %get-tuple-element.312), calls=%async_computation.5 | async-start | bytes 32768 | tf_op jit(solution)/shard_map/all_to_all | solution.py:181
Sparse Core Ops, SparseCore 0:
  9.6 51.1 all-gather.1
where the time goes:
time: 199 us
  waiting for transfers between devices  103 us (52%)
  starting transfers between devices  20.5 us (10%)
  other arithmetic  20.3 us (10%)
  blocking collectives  14.8 us (7%)
  between operations  14.3 us (7%)
  matrix products  13.9 us (7%)
  local copies, waits for them, and re-layouts  11.7 us (6%)
    all_gather x1, waiting for transfers between devices, local(): image_rows = lax.all_gather(descriptors, 'grp', axis=0, tiled=True)  52.2 us
    all_to_all x1, waiting for transfers between devices, in_one_piece(): lax.all_to_all(both, axis, split_axis=split_dim, concat_axis=concat_dim,...  32.2 us
    all_to_all x1, blocking collectives, in_one_piece(): lax.all_to_all(both, axis, split_axis=split_dim, concat_axis=concat_dim,...  11.1 us
    reduce_sum x2, other arithmetic, first_pass(): jnp.sum(jnp.where(key_mask, jnp.exp(scores - row_top[:, None]), 0.0), axi...  9.7 us
    dot_general x2, matrix products, first_pass(): jnp.einsum('qd,kd->qk', block_rows, key_image, preferred_element_type=jnp...  7.9 us
    all_to_all x1, starting transfers between devices, in_one_piece(): lax.all_to_all(both, axis, split_axis=split_dim, concat_axis=concat_dim,...  7.87 us
    all_to_all x1, waiting for transfers between devices, paired_blocks(): lax.all_to_all(to_owner(row_out), TILE, split_axis=0, concat_axis=0, tile...  7.06 us
    all_to_all x1, waiting for transfers between devices, exchange_in_order(): out = lax.all_to_all(out, axes[k], k, k, tiled=True)  6.28 us
  transfers between devices with their start and end apart: 5, of which 5 were waited for; matrix products, arithmetic and copies ran while one was open for 3% of the time, Pallas kernels for 0%

commit v1 on v0

--- a/solution.py
+++ b/solution.py
@@ -194,7 +194,9 @@
 
 def local(descriptors, pairs, counts):
     score_scale = 2.0 / math.sqrt(descriptors.shape[2])
-    image_rows = lax.all_gather(descriptors, "grp", axis=0, tiled=True)
+    image_rows = jnp.concatenate(
+        lax.all_to_all(jnp.stack([descriptors] * lax.axis_size("grp")), "grp", 0, 0), axis=0
+    )
     image_ids = lax.iota(jnp.int32, counts.shape[0])
     first_image = pairs[:, 0]
     second = pairs[:, 1]

time: 199 us -> 191 us (0.960)
  between operations: 14.3 us -> 0.94 us
  starting transfers between devices: 20.5 us -> 27.4 us
  waiting for transfers between devices: 103 us -> 98.8 us
  local copies, waits for them, and re-layouts: 11.7 us -> 15.4 us
    all_gather x1 -> x0, waiting for transfers between devices: 52.2 us -> none  [local(): image_rows = lax.all_gather(descriptors, 'grp', axis=0, tiled=True)]
    all_to_all x0 -> x1, waiting for transfers between devices: none -> 48.7 us  [local(): lax.all_to_all(jnp.stack([descriptors] * lax.axis_size('grp')), 'grp', 0, 0)]
    all_to_all x0 -> x1, starting transfers between devices: none -> 4.86 us  [local(): lax.all_to_all(jnp.stack([descriptors] * lax.axis_size('grp')), 'grp', 0, 0)]
    another operation x2 -> x3, local copies, waits for them, and re-layouts: 0.01 us -> 3.72 us  [the longest x1 3.71 us: local(): jnp.stack([descriptors] * lax.axis_size('grp'))]
    all_to_all x1, starting transfers between devices: 7.87 us -> 9.97 us  [in_one_piece(): lax.all_to_all(both, axis, split_axis=split_dim, concat_axis=concat_dim,...]
  transfers between devices with their start and end apart: 5 -> 5, of which waited for: 5 -> 5; matrix products, arithmetic and copies ran while one was open for 3% -> 2% of each run, Pallas kernels for 0% -> 0%
where the time goes in v1:
time: 191 us
  waiting for transfers between devices  98.8 us (52%)
  starting transfers between devices  27.4 us (14%)
  other arithmetic  19.5 us (10%)
  local copies, waits for them, and re-layouts  15.4 us (8%)
  blocking collectives  14.8 us (8%)
  matrix products  13.7 us (7%)
    all_to_all x1, waiting for transfers between devices, local(): lax.all_to_all(jnp.stack([descriptors] * lax.axis_size('grp')), 'grp', 0, 0)  48.7 us
    all_to_all x1, waiting for transfers between devices, in_one_piece(): lax.all_to_all(both, axis, split_axis=split_dim, concat_axis=concat_dim,...  32.2 us
    all_to_all x1, blocking collectives, in_one_piece(): lax.all_to_all(both, axis, split_axis=split_dim, concat_axis=concat_dim,...  11.1 us
    all_to_all x1, starting transfers between devices, in_one_piece(): lax.all_to_all(both, axis, split_axis=split_dim, concat_axis=concat_dim,...  9.97 us
    reduce_sum x2, other arithmetic, first_pass(): jnp.sum(jnp.where(key_mask, jnp.exp(scores - row_top[:, None]), 0.0), axi...  9.69 us
    dot_general x2, matrix products, first_pass(): jnp.einsum('qd,kd->qk', block_rows, key_image, preferred_element_type=jnp...  7.68 us
    all_to_all x1, waiting for transfers between devices, paired_blocks(): lax.all_to_all(to_owner(row_out), TILE, split_axis=0, concat_axis=0, tile...  7.06 us
    all_to_all x1, waiting for transfers between devices, exchange_in_order(): out = lax.all_to_all(out, axes[k], k, k, tiled=True)  6.28 us
  transfers between devices with their start and end apart: 5, of which 5 were waited for; matrix products, arithmetic and copies ran while one was open for 2% of the time, Pallas kernels for 0%

profile of v1, /device:TPU:1, one launch (start us, length us, event | category | flops | bytes accessed | tf_op | source)
XLA Modules:
  0.0 190.6 jit_solution(13784941173569258639)
XLA Ops:
  0.6 3.7 %stack.2 = bf16[4,16,128,256]{3,2,1,0:T(8,128)(2,1)} broadcast(bf16[16,128,256]{2,1,0:T(8,128)(2,1)} %param.9), dimensions={1,2,3} | broadcast | bytes 5242880 | tf_op jit(solution)/shard_map/stack | solution.py:198
  4.4 4.9 %all-to-all-start = ((bf16[4,16,128,256]{3,2,1,0:T(8,128)(2,1)}), bf16[4,16,128,256]{3,2,1,0:T(8,128)(2,1)}, u32[]{:S(2)}, u32[]{:S(2)}) async-start(bf16[4,16,128,256]{3,2,1,0:T(8,128)(2,1)} %stack.2), calls=%async_computation | async-start | bytes 8388608 | tf_op jit(solution)/shard_map/all_to_all | solution.py:198
  9.3 48.7 %all-to-all-done = bf16[4,16,128,256]{3,2,1,0:T(8,128)(2,1)} async-done(((bf16[4,16,128,256]{3,2,1,0:T(8,128)(2,1)}), bf16[4,16,128,256]{3,2,1,0:T(8,128)(2,1)}, u32[]{:S(2)}, u32[]{:S(2)}) %all-to-all-start) | async-done | bytes 4194336 | tf_op jit(solution)/shard_map/all_to_all | solution.py:198
  58.0 2.8 %gather_fusion = bf16[8,128,256]{2,1,0:T(8,128)(2,1)S(1)} fusion(bf16[64,128,256]{2,1,0:T(8,128)(2,1)} %bitcast.2, s32[1024]{0:T(1024)S(1)} %pad_clamp_fusion.1), kind=kCustom, calls=%fused_computation.clone | custom fusion | bytes 1048608 | tf_op jit(solution)/shard_map/jit(_take)/gather | solution.py:209
  60.8 2.8 %gather_fusion.1 = bf16[8,128,256]{2,1,0:T(8,128)(2,1)S(1)} fusion(bf16[64,128,256]{2,1,0:T(8,128)(2,1)} %bitcast.2, s32[1024]{0:T(1024)S(1)} %pad_clamp_fusion), kind=kCustom, calls=%fused_computation.1.clone | custom fusion | bytes 1048608 | tf_op jit(solution)/shard_map/jit(_take)/gather | solution.py:210
  63.5 0.2 broadcast_select_fusion
  63.7 0.2 broadcast_in_dim.140
  64.0 1.7 pad_maximum_fusion
  65.7 10.0 %all-to-all-start.1 = ((bf16[32,1,160,256]{3,2,1,0:T(8,128)(2,1)}), bf16[32,1,160,256]{3,2,1,0:T(8,128)(2,1)S(1)}, u32[]{:S(2)}, u32[]{:S(2)}) async-start(bf16[32,1,160,256]{3,2,1,0:T(8,128)(2,1)} %pad_maximum_fusion), calls=%async_computation.1 | async-start | bytes 5242880 | tf_op jit(solution)/shard_map/all_to_all | solution.py:16
  75.7 0.2 select_reduce_fusion.5
  75.9 0.6 dynamic_slice.52
  76.5 0.6 dynamic_slice.53
  77.2 0.1 add.160
  77.3 0.1 add.162
  77.4 32.2 %all-to-all-done.1 = bf16[32,1,160,256]{3,2,1,0:T(8,128)(2,1)S(1)} async-done(((bf16[32,1,160,256]{3,2,1,0:T(8,128)(2,1)}), bf16[32,1,160,256]{3,2,1,0:T(8,128)(2,1)S(1)}, u32[]{:S(2)}, u32[]{:S(2)}) %all-to-all-start.1) | async-done | bytes 2621472 | tf_op jit(solution)/shard_map/all_to_all | solution.py:16
  109.6 1.5 slice.61
  111.1 20.4 %while.48 = (s32[]{:T(128)}, f32[4096]{0:T(1024)S(1)}, f32[4096]{0:T(1024)S(1)}, f32[2,512]{1,0:T(2,128)S(1)}, s32[2,512]{1,0:T(2,128)S(1)}, /*index=5*/s32[]{:T...) while((s32[]{:T(128)}, f32[4096]{0:T(1024)S(1)}, ...), condition=%wide.region_7.9_spmd.clone, body=%wide.region_2.8_spmd.clone.sunk | while | flops 1098936320 | bytes 19316360 | solution.py:86
  111.2 0.7 compare_reduce_fusion.8
  111.8 0.7 compare_reduce_fusion.7
  112.5 3.8 %select_reduce_fusion.11 = (f32[512]{0:T(512)S(1)}, f32[4096]{0:T(1024)S(1)}, f32[512,4096]{1,0:T(8,128)S(1)}) fusion(pred[4096]{0:T(1024)(128)(4,1)S(1)} %compare_reduce_fusion.7, pred[512]{0:T(512)(128)(4,1)S(1)} %compare_reduce_fusion.8, bf16[4096,256]{1,0:T(8,128)(2,1)} %get-tuple-element.457, bf16[2,512,256]{2,1,0:T(8,128)(2,1)S(1)} %get-tuple-element.456, ...), kind=kOutput, calls=%fused_computation.11.clone.1 | convolution fusion | flops 1084222976 | bytes 10770948 | tf_op jit(solution)/shard_map/while/body/eval_jaxpr/while/body/eval_jaxpr/qd,kd->qk/dot_general | solution.py:72
  116.4 4.8 %select_reduce_fusion.12 = (f32[512]{0:T(512)S(1)}, f32[4096]{0:T(1024)S(1)}) fusion(f32[512,4096]{1,0:T(8,128)S(1)} %get-tuple-element.421, f32[512]{0:T(512)S(1)} %get-tuple-element.422, pred[4096]{0:T(1024)(128)(4,1)S(1)} %compare_reduce_fusion.7, f32[4096]{0:T(1024)S(1)} %get-tuple-element.423, pred[512]{0:T(512)(128)(4,1)S(1)} %compare_reduce_fusion.8), kind=kLoop, calls=%fused_computation.10.clone.1 | loop fusion | flops 14675456 | bytes 8430080 | tf_op jit(solution)/shard_map/while/body/eval_jaxpr/while/body/eval_jaxpr/reduce_sum | solution.py:77
  121.3 0.7 compare_reduce_fusion.8
  122.0 0.7 compare_reduce_fusion.7
  122.7 3.8 %select_reduce_fusion.11 = (f32[512]{0:T(512)S(1)}, f32[4096]{0:T(1024)S(1)}, f32[512,4096]{1,0:T(8,128)S(1)}) fusion(pred[4096]{0:T(1024)(128)(4,1)S(1)} %compare_reduce_fusion.7, pred[512]{0:T(512)(128)(4,1)S(1)} %compare_reduce_fusion.8, bf16[4096,256]{1,0:T(8,128)(2,1)} %get-tuple-element.457, bf16[2,512,256]{2,1,0:T(8,128)(2,1)S(1)} %get-tuple-element.456, ...), kind=kOutput, calls=%fused_computation.11.clone.1 | convolution fusion | flops 1084222976 | bytes 10770948 | tf_op jit(solution)/shard_map/while/body/eval_jaxpr/while/body/eval_jaxpr/qd,kd->qk/dot_general | solution.py:72
  126.6 4.8 %select_reduce_fusion.12 = (f32[512]{0:T(512)S(1)}, f32[4096]{0:T(1024)S(1)}) fusion(f32[512,4096]{1,0:T(8,128)S(1)} %get-tuple-element.421, f32[512]{0:T(512)S(1)} %get-tuple-element.422, pred[4096]{0:T(1024)(128)(4,1)S(1)} %compare_reduce_fusion.7, f32[4096]{0:T(1024)S(1)} %get-tuple-element.423, pred[512]{0:T(512)(128)(4,1)S(1)} %compare_reduce_fusion.8), kind=kLoop, calls=%fused_computation.10.clone.1 | loop fusion | flops 14675456 | bytes 8430080 | tf_op jit(solution)/shard_map/while/body/eval_jaxpr/while/body/eval_jaxpr/reduce_sum | solution.py:77
  131.5 11.1 %all_to_all.35 = f32[32,2,128]{2,1,0:T(2,128)S(1)} all-to-all(f32[32,2,128]{2,1,0:T(2,128)S(1)} %pad_maximum_fusion.1), channel_id=1, replica_groups=mesh['grp'=4,'tile_0'=4,'tile_1'=4,'tile_2'=2] {'tile_0','tile_1','tile_2'}, dimensions={0} | all-to-all | bytes 65536 | tf_op jit(solution)/shard_map/all_to_all | solution.py:16
  142.7 3.8 %all_to_all.36 = f32[16,2,1,1,128]{4,3,2,0,1:T(1,128)S(1)} all-to-all(f32[16,2,1,1,128]{4,3,2,0,1:T(1,128)S(1)} %broadcast_in_dim.147), channel_id=1, replica_groups=mesh['grp'=4,'tile_0'=4,'tile_1'=4,'tile_2'=2] {'tile_2'}, dimensions={1} | all-to-all | bytes 32768 | tf_op jit(solution)/shard_map/all_to_all | solution.py:42
  146.5 0.6 copy.102
  147.1 3.5 %all-to-all-start.5 = ((f32[16,2,1,1,128]{4,3,2,1,0:T(1,128)}), f32[16,2,1,1,128]{4,3,2,1,0:T(1,128)S(1)}, u32[]{:S(2)}, u32[]{:S(2)}) async-start(f32[16,2,1,1,128]{4,3,2,1,0:T(1,128)} %copy.102), calls=%async_computation.5 | async-start | bytes 32768 | tf_op jit(solution)/shard_map/all_to_all | solution.py:42
  150.6 0.1 squeeze.81
  150.7 6.3 %all-to-all-done.5 = f32[16,2,1,1,128]{4,3,2,1,0:T(1,128)S(1)} async-done(((f32[16,2,1,1,128]{4,3,2,1,0:T(1,128)}), f32[16,2,1,1,128]{4,3,2,1,0:T(1,128)S(1)}, u32[]{:S(2)}, u32[]{:S(2)}) %all-to-all-start.5) | async-done | bytes 16416 | tf_op jit(solution)/shard_map/all_to_all | solution.py:42
  157.0 7.6 %while.47 = (s32[]{:T(128)}, f32[2,512]{1,0:T(2,128)S(1)}, bf16[2,512,256]{2,1,0:T(8,128)(2,1)S(1)}, bf16[4096,256]{1,0:T(8,128)(2,1)}, f32[4096]{0:T(1024)S(1)}...) while((s32[]{:T(128)}, f32[2,512]{1,0:T(2,128)S(1)}, ...), condition=%wide.region_10.12_spmd.clone, body=%wide.region_8.11_spmd.clone.sunk | while | flops 1082134528 | bytes 2396269 | solution.py:113
  157.0 0.7 compare_reduce_fusion.6
  157.7 3.0 %select_reduce_fusion.10 = f32[512]{0:T(512)S(1)} fusion(bf16[4096,256]{1,0:T(8,128)(2,1)} %get-tuple-element.482, f32[4096]{0:T(1024)S(1)} %get-tuple-element.483, pred[4096]{0:T(1024)(128)(4,1)S(1)} %compare_reduce_fusion.6, bf16[2,512,256]{2,1,0:T(8,128)(2,1)S(1)} %get-tuple-element.481, s32[]{:T(128)} %get-tuple-element.470), kind=kOutput, calls=%fused_computation.4.clone.1 | convolution fusion | flops 1082129920 | bytes 2381828 | tf_op jit(solution)/shard_map/while/body/eval_jaxpr/while/body/eval_jaxpr/qd,kd->qk/dot_general | solution.py:104
  160.8 0.7 compare_reduce_fusion.6
  161.5 3.0 %select_reduce_fusion.10 = f32[512]{0:T(512)S(1)} fusion(bf16[4096,256]{1,0:T(8,128)(2,1)} %get-tuple-element.482, f32[4096]{0:T(1024)S(1)} %get-tuple-element.483, pred[4096]{0:T(1024)(128)(4,1)S(1)} %compare_reduce_fusion.6, bf16[2,512,256]{2,1,0:T(8,128)(2,1)S(1)} %get-tuple-element.481, s32[]{:T(128)} %get-tuple-element.470), kind=kOutput, calls=%fused_computation.4.clone.1 | convolution fusion | flops 1082129920 | bytes 2381828 | tf_op jit(solution)/shard_map/while/body/eval_jaxpr/while/body/eval_jaxpr/qd,kd->qk/dot_general | solution.py:104
  164.6 0.1 reshape.252
  164.7 1.4 compare_select_fusion
  166.0 4.9 %all-to-all-start.2 = ((f32[32,1,32]{2,1,0:T(1,128)}), f32[32,1,32]{2,1,0:T(1,128)S(1)}, u32[]{:S(2)}, u32[]{:S(2)}) async-start(f32[32,1,32]{2,1,0:T(1,128)} %get-tuple-element.313), calls=%async_computation.2 | async-start | bytes 32768 | tf_op jit(solution)/shard_map/all_to_all | solution.py:180
  171.0 7.1 %all-to-all-done.2 = f32[32,1,32]{2,1,0:T(1,128)S(1)} async-done(((f32[32,1,32]{2,1,0:T(1,128)}), f32[32,1,32]{2,1,0:T(1,128)S(1)}, u32[]{:S(2)}, u32[]{:S(2)}) %all-to-all-start.2) | async-done | bytes 4128 | tf_op jit(solution)/shard_map/all_to_all | solution.py:180
  178.0 4.2 %all-to-all-start.6 = ((f32[32,1,32]{2,1,0:T(1,128)}), f32[32,1,32]{2,1,0:T(1,128)S(1)}, u32[]{:S(2)}, u32[]{:S(2)}) async-start(f32[32,1,32]{2,1,0:T(1,128)} %get-tuple-element.312), calls=%async_computation.6 | async-start | bytes 32768 | tf_op jit(solution)/shard_map/all_to_all | solution.py:181
  182.2 0.7 add_select_fusion
  182.9 0.5 broadcast.201
  183.4 0.7 reduce.12
  184.1 0.7 reshape_transpose_reshape.10
  184.7 4.5 %all-to-all-done.6 = f32[32,1,32]{2,1,0:T(1,128)S(1)} async-done(((f32[32,1,32]{2,1,0:T(1,128)}), f32[32,1,32]{2,1,0:T(1,128)S(1)}, u32[]{:S(2)}, u32[]{:S(2)}) %all-to-all-start.6) | async-done | bytes 4128 | tf_op jit(solution)/shard_map/all_to_all | solution.py:181
  189.3 0.7 reduce.13
  190.0 0.7 reshape_transpose_reshape.11
  (36 shorter events, 0.6 us)
Async XLA Ops:
  0.6 8.6 %copy-start = (s32[8,2]{0,1:T(2,128)S(1)}, s32[8,2]{0,1:T(2,128)}, u32[]{:S(2)}) copy-start(s32[8,2]{0,1:T(2,128)} %param.10) | copy-start | bytes 196
  4.4 53.6 %all-to-all-start = ((bf16[4,16,128,256]{3,2,1,0:T(8,128)(2,1)}), bf16[4,16,128,256]{3,2,1,0:T(8,128)(2,1)}, u32[]{:S(2)}, u32[]{:S(2)}) async-start(bf16[4,16,128,256]{3,2,1,0:T(8,128)(2,1)} %stack.2), calls=%async_computation | async-start | bytes 8388608 | tf_op jit(solution)/shard_map/all_to_all | solution.py:198
  60.8 15.0 %copy-start.1 = (s32[64]{0:T(128)S(1)}, s32[64]{0:T(128)}, u32[]{:S(2)}) copy-start(s32[64]{0:T(128)} %param.11) | copy-start | bytes 772
  65.7 43.9 %all-to-all-start.1 = ((bf16[32,1,160,256]{3,2,1,0:T(8,128)(2,1)}), bf16[32,1,160,256]{3,2,1,0:T(8,128)(2,1)S(1)}, u32[]{:S(2)}, u32[]{:S(2)}) async-start(bf16[32,1,160,256]{3,2,1,0:T(8,128)(2,1)} %pad_maximum_fusion), calls=%async_computation.1 | async-start | bytes 5242880 | tf_op jit(solution)/shard_map/all_to_all | solution.py:16
  147.1 9.9 %all-to-all-start.5 = ((f32[16,2,1,1,128]{4,3,2,1,0:T(1,128)}), f32[16,2,1,1,128]{4,3,2,1,0:T(1,128)S(1)}, u32[]{:S(2)}, u32[]{:S(2)}) async-start(f32[16,2,1,1,128]{4,3,2,1,0:T(1,128)} %copy.102), calls=%async_computation.5 | async-start | bytes 32768 | tf_op jit(solution)/shard_map/all_to_all | solution.py:42
  166.0 12.0 %all-to-all-start.2 = ((f32[32,1,32]{2,1,0:T(1,128)}), f32[32,1,32]{2,1,0:T(1,128)S(1)}, u32[]{:S(2)}, u32[]{:S(2)}) async-start(f32[32,1,32]{2,1,0:T(1,128)} %get-tuple-element.313), calls=%async_computation.2 | async-start | bytes 32768 | tf_op jit(solution)/shard_map/all_to_all | solution.py:180
  178.0 11.2 %all-to-all-start.6 = ((f32[32,1,32]{2,1,0:T(1,128)}), f32[32,1,32]{2,1,0:T(1,128)S(1)}, u32[]{:S(2)}, u32[]{:S(2)}) async-start(f32[32,1,32]{2,1,0:T(1,128)} %get-tuple-element.312), calls=%async_computation.6 | async-start | bytes 32768 | tf_op jit(solution)/shard_map/all_to_all | solution.py:181
